TPU v7x, 32 devices: a whole 2x2x4 slice. The times are simulated.
32 devices in a mesh: dp: 8 (over z, x), feat: 4 (over y, core).
Axes of the slice: x: 2, y: 2, z: 4, core: 2. Of those that a mesh axis runs over, the one named last changes fastest.
Arguments:
- activations: bfloat16 [2048, 8192], P('dp', 'feat'), may hold values from -6 to 6
- cotangent: bfloat16 [2048, 1024], P('dp'), may hold values from -0.13183594 to 0.13183594
- weight: float32 [8192, 1024], P('feat'), may hold values from -0.0625 to 0.0625
- stats_old: float32 [4, 8, 4, 256, 256], P('feat', 'dp'), as said below
- owners: int32 [32, 4], replicated, may hold values from 0 to 7, as said below
- next_acts: bfloat16 [2048, 8192], P('dp', 'feat'), may hold values from -6 to 6
Outputs:
- weight_new: float32 [8192, 1024], P('feat')
- stats_new: float32 [4, 8, 4, 256, 256], P('feat', 'dp')
- next_out: bfloat16 [2048, 1024], P('dp', 'feat')
Inputs may be any that keep to these rules, and one draw needn't show every extreme that they name: `owners`: blocks are grouped by the index of feat that holds their rows (8192 / (256 * 4) row blocks a group); in every group each dp index owns at most 4 blocks, and some dp index owns exactly 4. `stats_old`: every slot holds a symmetric positive definite matrix; slots that no block maps to are not read.
All inputs are finite; a program needn't handle non-finite values.
Results may differ from a plain program's by a relative error of at most 0.02.
Values may be sent and summed in bfloat16 or wider, within the bound.
A program may use at most 128 MiB of HBM per device.

v0:
```python
import jax
import jax.numpy as jnp
from jax import lax
from jax.sharding import PartitionSpec as P

ITERS = 6


decay_rate = 0.9
step_rate = 0.01


def from_root(x, axis, root):
    mine = lax.axis_index(axis) == root
    return lax.psum(jnp.where(mine, x, jnp.zeros_like(x)), axis)


def newton_root(stats):
    width = stats.shape[0]
    identity = jnp.eye(width, dtype=jnp.float32)
    norm_value = jnp.sqrt(jnp.sum(stats * stats) + 1e-06)
    matrix = stats / norm_value
    iterate = identity
    for counter in range(ITERS):
        factor = (5.0 * identity - matrix) / 4.0
        factor_low = factor.astype(jnp.bfloat16)
        iterate = jnp.dot(
            iterate.astype(jnp.bfloat16), factor_low, preferred_element_type=jnp.float32
        )
        if counter + 1 < ITERS:
            square = jnp.dot(factor_low, factor_low, preferred_element_type=jnp.float32).astype(
                jnp.bfloat16
            )
            fourth = jnp.dot(square, square, preferred_element_type=jnp.float32).astype(
                jnp.bfloat16
            )
            matrix = jnp.dot(
                fourth, matrix.astype(jnp.bfloat16), preferred_element_type=jnp.float32
            )
    return iterate * norm_value ** (-0.25)


def update_stats(grad_block, old_stats):
    gram = (
        jnp.dot(grad_block, grad_block.T, preferred_element_type=jnp.float32) / grad_block.shape[0]
    )
    return decay_rate * old_stats + (1.0 - decay_rate) * gram


def block_at(matrix, block_id, col_blocks, width):
    row_start = block_id // col_blocks * width
    col_start = block_id % col_blocks * width
    return lax.dynamic_slice(matrix, (row_start, col_start), (width, width))


def body(activations, cotangent, weight, stats_old, owners, next_acts):
    width = stats_old.shape[-1]
    slots = stats_old.shape[2]
    rows_dev, columns = weight.shape
    row_blocks = rows_dev // width
    col_blocks = columns // width
    block_count = row_blocks * col_blocks
    partial_grad = jnp.einsum(
        "td,tc->dc", activations, cotangent, preferred_element_type=jnp.float32
    )
    summed = lax.psum(partial_grad, "dp")
    grad_low = summed.astype(jnp.bfloat16)
    feat_index = lax.axis_index("feat")
    data_index = lax.axis_index("dp")
    own_list = lax.dynamic_slice_in_dim(owners, feat_index * row_blocks, row_blocks, 0).reshape(
        block_count
    )
    is_mine = (own_list == data_index).astype(jnp.int32)
    slot_of = jnp.cumsum(is_mine) - is_mine
    block_ids = jnp.arange(block_count, dtype=jnp.int32)
    slot_pick = jnp.clip(slot_of, 0, slots - 1)
    stats_list = []
    renewed_list = []
    chosen_list = []
    for position in range(slots):
        picked = (is_mine == 1) & (slot_of == position)
        alive = jnp.any(picked)
        chosen = jnp.sum(jnp.where(picked, block_ids, 0))
        grad_block = block_at(grad_low, chosen, col_blocks, width)
        renewed = update_stats(grad_block, stats_old[0, 0, position])
        stats_list.append(jnp.where(alive, renewed, 0.0))
        renewed_list.append(renewed)
        chosen_list.append(chosen)
    root_list = [newton_root(renewed) for renewed in renewed_list]
    new_list = []
    fresh_list = []
    for root_matrix, chosen in zip(root_list, chosen_list):
        grad_block = block_at(grad_low, chosen, col_blocks, width)
        weight_block = block_at(weight, chosen, col_blocks, width)
        update = jnp.dot(
            root_matrix.astype(jnp.bfloat16), grad_block, preferred_element_type=jnp.float32
        )
        fresh_list.append(weight_block - step_rate * update)
    candidates = jnp.stack(fresh_list)
    for position in range(block_count):
        sending = lax.dynamic_index_in_dim(candidates, slot_pick[position], 0, keepdims=False)
        new_list.append(
            from_root(sending.astype(jnp.bfloat16), "dp", own_list[position]).astype(sending.dtype)
        )
    new_blocks = jnp.stack(new_list)
    weight_new = (
        new_blocks.reshape(row_blocks, col_blocks, width, width)
        .transpose(0, 2, 1, 3)
        .reshape(rows_dev, columns)
    )
    stats_out = jnp.stack(stats_list)[None, None]
    partial_next = jnp.dot(
        next_acts, weight_new.astype(jnp.bfloat16), preferred_element_type=jnp.float32
    )
    next_out = lax.psum_scatter(
        partial_next.astype(jnp.bfloat16), "feat", scatter_dimension=1, tiled=True
    )
    return (weight_new, stats_out, next_out)


def solution(mesh):
    placed = (
        P("dp", "feat"),
        P("dp", None),
        P("feat", None),
        P("feat", "dp", None, None, None),
        P(),
        P("dp", "feat"),
    )
    return jax.shard_map(
        body,
        mesh=mesh,
        in_specs=placed,
        out_specs=(P("feat", None), P("feat", "dp", None, None, None), P("dp", "feat")),
        check_vma=False,
    )
```

profile of v0, /device:TPU:0, one launch (start us, length us, event | category | flops | bytes accessed | tf_op | source)
XLA Modules:
  0.0 700.2 jit_solution(15082206161460627291)
XLA Ops:
  7.2 0.8 constant_dynamic-slice_fusion
  13.1 5.7 fusion.363
  18.9 328.1 %all-reduce.5 = bf16[2048,1024]{1,0:T(8,128)(2,1)} all-reduce(f32[2048,1024]{1,0:T(8,128)} %fusion.363), channel_id=1, replica_groups=mesh['dp'=8,'feat'=4] {'dp'}, use_global_device_ids=true, to_apply=%region_2.3 | all-reduce | flops 2097152 | bytes 12582912 | tf_op jit(solution)/shard_map/psum | solution.py:66
  347.0 1.8 multiply_reduce_fusion
  351.3 1.0 convolution_convert_fusion.12
  354.6 1.9 multiply_reduce_fusion.1
  358.9 1.0 convolution_convert_fusion.27
  363.3 1.8 multiply_reduce_fusion.2
  367.5 1.0 convolution_convert_fusion.42
  370.8 1.8 multiply_reduce_fusion.3
  373.3 0.7 select_bitcast_fusion.3
  375.2 1.0 convolution_convert_fusion.57
  384.1 0.7 fusion.360
  386.2 0.7 fusion.359
  421.7 1.2 convolution_convert_fusion.6
  425.8 1.2 fusion.2
  427.3 1.2 fusion.6
  431.4 1.2 fusion.10
  435.4 1.2 fusion.14
  476.9 0.8 fusion.69
  477.7 1.0 fusion.78
  478.7 1.1 fusion.87
  479.8 1.1 fusion.96
  481.2 166.1 %all-reduce.4.cloned.1.call-done = (bf16[1,256,256]{2,1,0:T(8,128)(2,1)}, bf16[1,256,256]{2,1,0:T(8,128)(2,1)}, bf16[1,256,256]{2,1,0:T(8,128)(2,1)}, bf16[1,256...) async-done(((bf16[1,256,256]{2,1,0:T(8,128)(2,1)}, ...) | async-done | bytes 4194320 | tf_op jit(solution)/shard_map/psum | solution.py:15
  647.4 1.1 constant_dynamic-update-slice_fusion.31
  648.5 0.9 constant_dynamic-update-slice_fusion.30
  649.4 0.9 constant_dynamic-update-slice_fusion.29
  650.3 0.9 constant_dynamic-update-slice_fusion.28
  651.2 0.9 constant_dynamic-update-slice_fusion.27
  652.1 0.9 constant_dynamic-update-slice_fusion.26
  653.0 0.9 constant_dynamic-update-slice_fusion.25
  654.0 0.9 constant_dynamic-update-slice_fusion.24
  654.9 0.9 constant_dynamic-update-slice_fusion.23
  655.8 0.9 constant_dynamic-update-slice_fusion.22
  656.7 0.9 constant_dynamic-update-slice_fusion.21
  657.6 0.9 constant_dynamic-update-slice_fusion.20
  658.6 0.9 constant_dynamic-update-slice_fusion.19
  659.5 0.9 constant_dynamic-update-slice_fusion.18
  660.4 0.9 constant_dynamic-update-slice_fusion.17
  661.3 0.9 constant_dynamic-update-slice_fusion.16
  662.7 3.2 copy.15
  665.9 1.0 copy.18
  667.0 1.9 copy-done.2
  668.9 2.1 fusion
  671.1 1.0 maximum_bitcast_fusion
  672.1 6.6 reshape.195
  678.8 12.9 %reduce-scatter.2.cloned.1.call-done = bf16[256,256]{0,1:T(8,128)(2,1)} async-done(((bf16[256,1024]{0,1:T(8,128)(2,1)}), bf16[256,256]{0,1:T(8,128)(2,1)}) %reduce-scatter.2.cloned.1.call-update) | async-done | bytes 131088 | tf_op jit(solution)/shard_map/reduce_scatter | solution.py:115
  691.7 1.7 copy.16
  (132 shorter events, 22.2 us)
Async XLA Ops:
  7.2 6.0 copy-start
  7.2 640.1 %all-reduce.4.cloned.1.call-start = ((), (), s32[]{:S(2)}) async-start(), calls=%async_computation.2 | async-start | bytes 8388608 | tf_op jit(solution)/shard_map/psum | solution.py:15
  18.9 328.1 %copy-start.3 = (f32[1,1,4,256,256]{4,3,2,1,0:T(8,128)S(1)}, f32[1,1,4,256,256]{4,3,2,1,0:T(8,128)}, u32[]{:S(2)}) copy-start(f32[1,1,4,256,256]{4,3,2,1,0:T(8,128)} %param.9) | copy-start | bytes 3145732
  419.7 5.3 copy-start.21
  425.4 5.3 copy-start.22
  429.4 5.3 copy-start.23
  480.9 210.8 %reduce-scatter.2.cloned.1.call-start = ((), (), s32[]{:S(2)}) async-start(), calls=%async_computation.1 | async-start | bytes 655360 | tf_op jit(solution)/shard_map/reduce_scatter | solution.py:115
  647.3 15.0 %copy-start.19 = (bf16[1,256,256]{2,1,0:T(8,128)(2,1)S(1)}, bf16[1,256,256]{2,1,0:T(8,128)(2,1)}, u32[]{:S(2)}) copy-start(bf16[1,256,256]{2,1,0:T(8,128)(2,1)} %get-tuple-element.25) | copy-start | bytes 393220
  647.3 15.0 %copy-start.18 = (bf16[1,256,256]{2,1,0:T(8,128)(2,1)S(1)}, bf16[1,256,256]{2,1,0:T(8,128)(2,1)}, u32[]{:S(2)}) copy-start(bf16[1,256,256]{2,1,0:T(8,128)(2,1)} %get-tuple-element.26) | copy-start | bytes 393220
  647.3 15.0 %copy-start.17 = (bf16[1,256,256]{2,1,0:T(8,128)(2,1)S(1)}, bf16[1,256,256]{2,1,0:T(8,128)(2,1)}, u32[]{:S(2)}) copy-start(bf16[1,256,256]{2,1,0:T(8,128)(2,1)} %get-tuple-element.27) | copy-start | bytes 393220
  647.3 15.0 %copy-start.16 = (bf16[1,256,256]{2,1,0:T(8,128)(2,1)S(1)}, bf16[1,256,256]{2,1,0:T(8,128)(2,1)}, u32[]{:S(2)}) copy-start(bf16[1,256,256]{2,1,0:T(8,128)(2,1)} %get-tuple-element.28) | copy-start | bytes 393220
  647.3 15.1 %copy-start.15 = (bf16[1,256,256]{2,1,0:T(8,128)(2,1)S(1)}, bf16[1,256,256]{2,1,0:T(8,128)(2,1)}, u32[]{:S(2)}) copy-start(bf16[1,256,256]{2,1,0:T(8,128)(2,1)} %get-tuple-element.29) | copy-start | bytes 393220
  647.3 15.1 %copy-start.14 = (bf16[1,256,256]{2,1,0:T(8,128)(2,1)S(1)}, bf16[1,256,256]{2,1,0:T(8,128)(2,1)}, u32[]{:S(2)}) copy-start(bf16[1,256,256]{2,1,0:T(8,128)(2,1)} %get-tuple-element.30) | copy-start | bytes 393220
  647.3 15.1 %copy-start.13 = (bf16[1,256,256]{2,1,0:T(8,128)(2,1)S(1)}, bf16[1,256,256]{2,1,0:T(8,128)(2,1)}, u32[]{:S(2)}) copy-start(bf16[1,256,256]{2,1,0:T(8,128)(2,1)} %get-tuple-element.31) | copy-start | bytes 393220
  647.3 15.1 %copy-start.12 = (bf16[1,256,256]{2,1,0:T(8,128)(2,1)S(1)}, bf16[1,256,256]{2,1,0:T(8,128)(2,1)}, u32[]{:S(2)}) copy-start(bf16[1,256,256]{2,1,0:T(8,128)(2,1)} %get-tuple-element.32) | copy-start | bytes 393220
  647.3 15.2 %copy-start.11 = (bf16[1,256,256]{2,1,0:T(8,128)(2,1)S(1)}, bf16[1,256,256]{2,1,0:T(8,128)(2,1)}, u32[]{:S(2)}) copy-start(bf16[1,256,256]{2,1,0:T(8,128)(2,1)} %get-tuple-element.33) | copy-start | bytes 393220
  647.3 15.2 %copy-start.10 = (bf16[1,256,256]{2,1,0:T(8,128)(2,1)S(1)}, bf16[1,256,256]{2,1,0:T(8,128)(2,1)}, u32[]{:S(2)}) copy-start(bf16[1,256,256]{2,1,0:T(8,128)(2,1)} %get-tuple-element.34) | copy-start | bytes 393220
  647.3 15.2 %copy-start.9 = (bf16[1,256,256]{2,1,0:T(8,128)(2,1)S(1)}, bf16[1,256,256]{2,1,0:T(8,128)(2,1)}, u32[]{:S(2)}) copy-start(bf16[1,256,256]{2,1,0:T(8,128)(2,1)} %get-tuple-element.35) | copy-start | bytes 393220
  647.3 15.2 %copy-start.8 = (bf16[1,256,256]{2,1,0:T(8,128)(2,1)S(1)}, bf16[1,256,256]{2,1,0:T(8,128)(2,1)}, u32[]{:S(2)}) copy-start(bf16[1,256,256]{2,1,0:T(8,128)(2,1)} %get-tuple-element.36) | copy-start | bytes 393220
  647.3 15.2 %copy-start.7 = (bf16[1,256,256]{2,1,0:T(8,128)(2,1)S(1)}, bf16[1,256,256]{2,1,0:T(8,128)(2,1)}, u32[]{:S(2)}) copy-start(bf16[1,256,256]{2,1,0:T(8,128)(2,1)} %get-tuple-element.37) | copy-start | bytes 393220
  647.4 15.2 %copy-start.6 = (bf16[1,256,256]{2,1,0:T(8,128)(2,1)S(1)}, bf16[1,256,256]{2,1,0:T(8,128)(2,1)}, u32[]{:S(2)}) copy-start(bf16[1,256,256]{2,1,0:T(8,128)(2,1)} %get-tuple-element.38) | copy-start | bytes 393220
  647.4 15.3 %copy-start.5 = (bf16[1,256,256]{2,1,0:T(8,128)(2,1)S(1)}, bf16[1,256,256]{2,1,0:T(8,128)(2,1)}, u32[]{:S(2)}) copy-start(bf16[1,256,256]{2,1,0:T(8,128)(2,1)} %get-tuple-element.39) | copy-start | bytes 393220
  647.4 15.3 %copy-start.4 = (bf16[1,256,256]{2,1,0:T(8,128)(2,1)S(1)}, bf16[1,256,256]{2,1,0:T(8,128)(2,1)}, u32[]{:S(2)}) copy-start(bf16[1,256,256]{2,1,0:T(8,128)(2,1)} %get-tuple-element.40) | copy-start | bytes 393220
  665.9 3.0 copy-start.20
  667.0 1.9 copy-start.2
  671.1 22.2 %copy-start.1 = (bf16[256,2048]{1,0:T(8,128)(2,1)S(1)}, bf16[256,2048]{1,0:T(8,128)(2,1)}, u32[]{:S(2)}) copy-start(bf16[256,2048]{1,0:T(8,128)(2,1)} %param.6) | copy-start | bytes 3145732
Sparse Core Ops, SparseCore 0:
  481.0 166.2 all-reduce.3
  671.2 20.4 reduce-scatter.1
where the time goes:
time: 702 us; the launch traced here: 700 us
  blocking collectives  328 us (47%)
  waiting for transfers between devices  179 us (25%)
  between operations  108 us (15%)
  matrix products  40.3 us (6%)
  local copies, waits for them, and re-layouts  27 us (4%)
  other arithmetic  17.4 us (2%)
    psum x1, blocking collectives, body(): summed = lax.psum(partial_grad, 'dp')  328 us
    psum x1, waiting for transfers between devices, from_root(): return lax.psum(jnp.where(mine, x, jnp.zeros_like(x)), axis)  166 us
    unnamed x82, local copies, waits for them, and re-layouts  19.8 us
  transfers between devices with their start and end apart: 2, of which 2 were waited for; matrix products, arithmetic and copies ran while one was open for 1% of the time, Pallas kernels for 0%

commit v1 on v0

v1 whole, which is shorter than its diff:
```python
import functools

import jax
import jax.numpy as jnp
from jax import lax
from jax.experimental import pallas as pl
from jax.experimental.pallas import tpu as pltpu
from jax.sharding import PartitionSpec as P

ITERS = 6
CHUNKS = 1

decay_rate = 0.9
step_rate = 0.01
VMEM_BYTES = 48 * 1024 * 1024


def grad_kernel(width, col_blocks, per_step, order_ref, act_ref, cot_ref, out_ref):
    base = pl.program_id(0) * per_step
    for j in range(per_step):
        block = order_ref[base + j]
        rows = pl.ds(pl.multiple_of(block // col_blocks * width, width), width)
        cols = pl.ds(pl.multiple_of(block % col_blocks * width, width), width)
        out_ref[j] = lax.dot_general(
            act_ref[:, rows],
            cot_ref[:, cols],
            (((0,), (0,)), ((), ())),
            preferred_element_type=jnp.float32,
        ).astype(out_ref.dtype)


def permuted_grad(order, activations, cotangent, width):
    total = order.shape[0]
    tokens, rows = activations.shape
    cols = cotangent.shape[1]
    per_step = 4 if total % 4 == 0 else 1
    return pl.pallas_call(
        functools.partial(grad_kernel, width, cols // width, per_step),
        out_shape=jax.ShapeDtypeStruct((total, width, width), jnp.bfloat16),
        grid_spec=pltpu.PrefetchScalarGridSpec(
            num_scalar_prefetch=1,
            grid=(total // per_step,),
            in_specs=[
                pl.BlockSpec((tokens, rows), lambda i, o: (0, 0)),
                pl.BlockSpec((tokens, cols), lambda i, o: (0, 0)),
            ],
            out_specs=pl.BlockSpec((per_step, width, width), lambda i, o: (i, 0, 0)),
        ),
        compiler_params=pltpu.CompilerParams(vmem_limit_bytes=VMEM_BYTES),
        cost_estimate=pl.CostEstimate(
            flops=2 * total * width * width * tokens,
            bytes_accessed=2 * (tokens * (rows + cols) + total * width * width),
            transcendentals=0,
        ),
        name="permuted_grad",
    )(order, activations, cotangent)


def newton_kernel(slots, width, alive_ref, grad_ref, old_ref, stats_ref, update_ref, mat_ref, iter_ref):
    row = lax.broadcasted_iota(jnp.int32, (width, width), 0)
    col = lax.broadcasted_iota(jnp.int32, (width, width), 1)
    identity = jnp.where(row == col, 1.0, 0.0).astype(jnp.float32)
    dot = functools.partial(jnp.dot, preferred_element_type=jnp.float32)
    norms = []
    for k in range(slots):
        g = grad_ref[k]
        gram = (
            lax.dot_general(g, g, (((1,), (1,)), ((), ())), preferred_element_type=jnp.float32)
            / width
        )
        renewed = decay_rate * old_ref[k] + (1.0 - decay_rate) * gram
        stats_ref[k] = jnp.where(alive_ref[k] > 0, renewed, 0.0)
        norm = jnp.sqrt(jnp.sum(renewed * renewed, keepdims=True) + 1e-06)
        norms.append(norm)
        mat_ref[k] = renewed / norm

    def factors():
        return [((5.0 * identity - mat_ref[k]) / 4.0).astype(jnp.bfloat16) for k in range(slots)]

    def advance(low):
        square = [dot(low[k], low[k]).astype(jnp.bfloat16) for k in range(slots)]
        fourth = [dot(square[k], square[k]).astype(jnp.bfloat16) for k in range(slots)]
        for k in range(slots):
            mat_ref[k] = dot(fourth[k], mat_ref[k].astype(jnp.bfloat16))

    low = factors()
    for k in range(slots):
        iter_ref[k] = low[k]
    advance(low)

    @pl.loop(1, ITERS - 1)
    def _(step):
        low = factors()
        for k in range(slots):
            iter_ref[k] = dot(iter_ref[k], low[k]).astype(jnp.bfloat16)
        advance(low)

    low = factors()
    for k in range(slots):
        root = dot(iter_ref[k], low[k]) * norms[k] ** (-0.25)
        update_ref[k] = dot(root.astype(jnp.bfloat16), grad_ref[k]).astype(jnp.bfloat16)


def newton(alive, grad, old):
    slots, width, _ = grad.shape
    vmem = pl.BlockSpec(memory_space=pltpu.VMEM)
    return pl.pallas_call(
        functools.partial(newton_kernel, slots, width),
        out_shape=(
            jax.ShapeDtypeStruct((slots, width, width), jnp.float32),
            jax.ShapeDtypeStruct((slots, width, width), jnp.bfloat16),
        ),
        in_specs=[pl.BlockSpec(memory_space=pltpu.SMEM), vmem, vmem],
        out_specs=(vmem, vmem),
        scratch_shapes=[
            pltpu.VMEM((slots, width, width), jnp.float32),
            pltpu.VMEM((slots, width, width), jnp.bfloat16),
        ],
        compiler_params=pltpu.CompilerParams(vmem_limit_bytes=VMEM_BYTES),
        cost_estimate=pl.CostEstimate(
            flops=2 * slots * 23 * width**3,
            bytes_accessed=slots * width * width * 12,
            transcendentals=0,
        ),
        name="newton",
    )(alive, grad, old)


def apply_kernel(width, col_blocks, chunks, place_ref, weight_ref, acts_ref, *refs):
    gathered = refs[:chunks]
    new_ref, part_ref, acc_ref = refs[chunks:]
    r = pl.program_id(0)

    @pl.when(r == 0)
    def _():
        acc_ref[...] = jnp.zeros_like(acc_ref)

    for c in range(col_blocks):
        cols = slice(c * width, (c + 1) * width)
        which = place_ref[0, r * col_blocks + c]
        index = place_ref[1, r * col_blocks + c]
        update = gathered[0][index]
        for n in range(1, chunks):
            update = jnp.where(which == n, gathered[n][index], update)
        fresh = weight_ref[:, cols] - step_rate * update.astype(jnp.float32)
        new_ref[:, cols] = fresh
        acc_ref[:, cols] += jnp.dot(
            acts_ref[...], fresh.astype(jnp.bfloat16), preferred_element_type=jnp.float32
        )

    @pl.when(r == pl.num_programs(0) - 1)
    def _():
        part_ref[...] = acc_ref[...].astype(part_ref.dtype)


def apply_update(place, weight, acts, gathered):
    width = gathered[0].shape[-1]
    rows, cols = weight.shape
    tokens = acts.shape[0]
    return pl.pallas_call(
        functools.partial(apply_kernel, width, cols // width, len(gathered)),
        out_shape=(
            jax.ShapeDtypeStruct((rows, cols), jnp.float32),
            jax.ShapeDtypeStruct((tokens, cols), jnp.bfloat16),
        ),
        grid_spec=pltpu.PrefetchScalarGridSpec(
            num_scalar_prefetch=1,
            grid=(rows // width,),
            in_specs=[
                pl.BlockSpec((width, cols), lambda i, p: (i, 0)),
                pl.BlockSpec((tokens, width), lambda i, p: (0, i)),
            ]
            + [pl.BlockSpec(g.shape, lambda i, p: (0, 0, 0), pipeline_mode=pl.Buffered(1)) for g in gathered],
            out_specs=(
                pl.BlockSpec((width, cols), lambda i, p: (i, 0)),
                pl.BlockSpec((tokens, cols), lambda i, p: (0, 0)),
            ),
            scratch_shapes=[pltpu.VMEM((tokens, cols), jnp.float32)],
        ),
        compiler_params=pltpu.CompilerParams(vmem_limit_bytes=VMEM_BYTES),
        cost_estimate=pl.CostEstimate(
            flops=2 * rows * cols * tokens,
            bytes_accessed=8 * rows * cols + 2 * sum(g.size for g in gathered),
            transcendentals=0,
        ),
        name="apply_update",
    )(place, weight, acts, *gathered)


def body(n_dp, activations, cotangent, weight, stats_old, owners, next_acts):
    width = stats_old.shape[-1]
    slots = stats_old.shape[2]
    rows_dev, columns = weight.shape
    row_blocks = rows_dev // width
    col_blocks = columns // width
    block_count = row_blocks * col_blocks
    chunks = CHUNKS if slots % CHUNKS == 0 else 1
    per = slots // chunks
    feat_index = lax.axis_index("feat")
    data_index = lax.axis_index("dp")
    own_list = lax.dynamic_slice_in_dim(owners, feat_index * row_blocks, row_blocks, 0).reshape(
        block_count
    )
    ids = jnp.arange(block_count, dtype=jnp.int32)
    slot_of = jnp.sum(
        ((own_list[:, None] == own_list[None, :]) & (ids[None, :] < ids[:, None])).astype(jnp.int32),
        axis=1,
    )
    chunk_of = slot_of // per
    index_of = own_list * per + slot_of % per
    place = jnp.stack([chunk_of, index_of])
    flat = chunk_of * (n_dp * per) + index_of
    held = flat[None, :] == jnp.arange(n_dp * slots, dtype=jnp.int32)[:, None]
    order = jnp.sum(jnp.where(held, ids[None, :], 0), axis=1)
    taken = jnp.sum(
        ((own_list == data_index)[None, :] & (slot_of[None, :] == jnp.arange(slots)[:, None])).astype(
            jnp.int32
        ),
        axis=1,
    )
    old = stats_old[0, 0]
    sums = []
    for n in range(chunks):
        part = permuted_grad(
            order[n * n_dp * per : (n + 1) * n_dp * per], activations, cotangent, width
        )
        sums.append(lax.psum_scatter(part, "dp", scatter_dimension=0, tiled=True))
    stats_list, gathered = [], []
    for n in range(chunks):
        span = slice(n * per, (n + 1) * per)
        stats, update = newton(taken[span], sums[n], old[span])
        stats_list.append(stats)
        gathered.append(lax.all_gather(update, "dp", axis=0, tiled=True))
    weight_new, partial_next = apply_update(place, weight, next_acts, gathered)
    stats_out = stats_list[0] if chunks == 1 else jnp.concatenate(stats_list)
    next_out = lax.psum_scatter(partial_next, "feat", scatter_dimension=1, tiled=True)
    return (weight_new, stats_out[None, None], next_out)


def solution(mesh):
    placed = (
        P("dp", "feat"),
        P("dp", None),
        P("feat", None),
        P("feat", "dp", None, None, None),
        P(),
        P("dp", "feat"),
    )
    return jax.shard_map(
        functools.partial(body, mesh.shape["dp"]),
        mesh=mesh,
        in_specs=placed,
        out_specs=(P("feat", None), P("feat", "dp", None, None, None), P("dp", "feat")),
        check_vma=False,
    )
```

time: 702 us -> 228 us (0.32)
  blocking collectives: 328 us -> 0 us
  between operations: 108 us -> 13.8 us
  matrix products: 40.3 us -> 0 us
  Pallas kernels: 0 us -> 21.1 us
  local copies, waits for them, and re-layouts: 27 us -> 7.84 us
  other arithmetic: 17.4 us -> 1.21 us
    psum x1 -> x0, blocking collectives: 328 us -> none  [body(): summed = lax.psum(partial_grad, 'dp')]
    psum x1 -> x0, waiting for transfers between devices: 166 us -> none  [from_root(): return lax.psum(jnp.where(mine, x, jnp.zeros_like(x)), axis)]
    reduce_scatter x1 -> x2, waiting for transfers between devices: 12.9 us -> 111 us  [the longest x1 91.1 us: body(): sums.append(lax.psum_scatter(part, 'dp', scatter_dimension=0, tiled=True))]
    all_gather x0 -> x1, waiting for transfers between devices: none -> 72.3 us  [body(): gathered.append(lax.all_gather(update, 'dp', axis=0, tiled=True))]
    dot_general x62 -> x0, matrix products: 40.3 us -> none  [the longest x20 8.85 us: newton_root(): jnp.dot(square, square, preferred_element_type=jnp.float32)]
    pallas_call x0 -> x3, Pallas kernels: none -> 21.1 us  [the longest x1 10.7 us: apply_update(): pl.pallas_call(functools.partial(apply_kernel, width, cols // width, len(...]
    unnamed x82 -> x14, local copies, waits for them, and re-layouts: 19.8 us -> 7.51 us
  transfers between devices with their start and end apart: 2 -> 3, of which waited for: 2 -> 3; matrix products, arithmetic and copies ran while one was open for 1% -> 0% of each run, Pallas kernels for 0% -> 0%
where the time goes in v1:
time: 228 us
  waiting for transfers between devices  184 us (81%)
  Pallas kernels  21.1 us (9%)
  between operations  13.8 us (6%)
  local copies, waits for them, and re-layouts  7.84 us (3%)
    reduce_scatter x1, waiting for transfers between devices, body(): sums.append(lax.psum_scatter(part, 'dp', scatter_dimension=0, tiled=True))  91.1 us
    all_gather x1, waiting for transfers between devices, body(): gathered.append(lax.all_gather(update, 'dp', axis=0, tiled=True))  72.3 us
    reduce_scatter x1, waiting for transfers between devices, body(): lax.psum_scatter(partial_next, 'feat', scatter_dimension=1, tiled=True)  20.4 us
    pallas_call x1, Pallas kernels, apply_update(): pl.pallas_call(functools.partial(apply_kernel, width, cols // width, len(...  10.7 us
    unnamed x14, local copies, waits for them, and re-layouts  7.51 us
    pallas_call x1, Pallas kernels, newton(): pl.pallas_call(functools.partial(newton_kernel, slots, width), out_shape=...  6.59 us
  transfers between devices with their start and end apart: 3, of which 3 were waited for; matrix products, arithmetic and copies ran while one was open for 0% of the time, Pallas kernels for 0%

profile of v1, /device:TPU:0, one launch (start us, length us, event | category | flops | bytes accessed | tf_op | source)
XLA Modules:
  0.0 227.9 jit_solution(11025814052105044187)
XLA Ops:
  7.2 0.0 reduce-scatter.3.cloned.1.call-start
  7.2 0.8 broadcast_multiply_fusion
  8.0 0.1 copy.15
  8.1 0.1 eq.51
  8.1 0.2 convert_reduce_fusion
  8.3 0.1 select_reduce_fusion.order_ref
  8.5 0.0 copy-start.2
  8.5 1.2 copy-done.2
  9.7 0.0 copy-start.4
  9.7 1.0 copy-done.4
  10.7 0.0 copy-start.5
  10.7 3.8 %permuted_grad.1 = bf16[32,256,256]{2,1,0:T(8,128)(2,1)S(1)} custom-call(s32[32]{0:T(128)S(1)} %select_reduce_fusion.order_ref, bf16[256,2048]{1,0:T(8,128)(2,1)S(1)} %copy-done.2, bf16[256,1024]{1,0:T(8,128)(2,1)S(1)} %copy-done.4), custom_call_target="tpu_custom_call" | custom-call | flops 1073741824 | bytes 5767168 | tf_op jit(solution)/shard_map/permuted_grad/pallas_call | solution.py:37
  14.5 0.0 copy-start
  14.5 2.0 copy-done
  16.5 0.0 copy-start.3
  16.5 0.0 reduce-scatter.3.cloned.1.call-update
  16.5 0.0 all-gather.2.cloned.1.call-start
  16.6 0.1 convert_reduce_fusion.1.alive_ref
  16.7 91.1 %reduce-scatter.3.cloned.1.call-done.grad_ref = bf16[4,256,256]{2,1,0:T(8,128)(2,1)} async-done(((bf16[32,256,256]{2,1,0:T(8,128)(2,1)}), bf16[4,256,256]{2,1,0:T(8,128)(2,1)}) %reduce-scatter.3.cloned.1.call-update) | async-done | bytes 524304 | tf_op jit(solution)/shard_map/reduce_scatter | solution.py:227
  107.8 0.0 copy-done.5
  107.8 0.0 copy-start.6
  107.8 1.0 copy-done.6
  108.9 6.6 %newton.1 = (f32[4,256,256]{2,1,0:T(8,128)}, bf16[4,256,256]{2,1,0:T(8,128)(2,1)}) custom-call(s32[4]{0:T(128)S(1)} %convert_reduce_fusion.1.alive_ref, bf16[4,256,256]{2,1,0:T(8,128)(2,1)S(1)} %copy-done.6, f32[4,256,256]{2,1,0:T(8,128)S(1)} %bitcast.17), custom_call_target="tpu_custom_call" | custom-call | flops 3087007744 | bytes 3145728 | tf_op jit(solution)/shard_map/newton/pallas_call | solution.py:107
  115.5 0.0 all-gather.2.cloned.1.call-update
  115.5 0.0 reduce-scatter.5.cloned.1.call-start
  115.5 0.1 copy.16
  115.6 0.1 mul.34
  115.7 72.3 %all-gather.2.cloned.1.call-done.refs_0_ = bf16[32,256,256]{2,1,0:T(8,128)(2,1)} async-done(((bf16[4,256,256]{2,1,0:T(8,128)(2,1)}), bf16[32,256,256]{2,1,0:T(8,128)(2,1)}) %all-gather.2.cloned.1.call-update) | async-done | bytes 4194320 | tf_op jit(solution)/shard_map/all_gather | solution.py:233
  188.1 0.0 copy-done.3
  188.1 0.0 copy-start.1
  188.1 2.2 copy-done.1
  190.3 10.7 %apply_update.1 = (f32[2048,1024]{1,0:T(8,128)}, bf16[256,1024]{1,0:T(8,128)(2,1)}) custom-call(s32[2,32]{1,0:T(2,128)S(1)} %pad_add_fusion.place_ref, f32[2048,1024]{1,0:T(8,128)} %weight_ref.1, bf16[256,2048]{1,0:T(8,128)(2,1)S(1)} %copy-done.3, bf16[32,256,256]{2,1,0:T(8,128)(2,1)S(1)} %copy-done.1), custom_call_target="tpu_custom_call" | custom-call | flops 1073741824 | bytes 20971520 | tf_op jit(solution)/shard_map/apply_update/pallas_call | solution.py:160
  201.0 0.0 reduce-scatter.5.cloned.1.call-update
  201.0 20.4 %reduce-scatter.5.cloned.1.call-done = bf16[256,256]{1,0:T(8,128)(2,1)} async-done(((bf16[256,1024]{1,0:T(8,128)(2,1)}), bf16[256,256]{1,0:T(8,128)(2,1)}) %reduce-scatter.5.cloned.1.call-update) | async-done | bytes 131088 | tf_op jit(solution)/shard_map/reduce_scatter | solution.py:236
  (4 shorter events, 0.0 us)
Async XLA Ops:
  7.2 100.7 %reduce-scatter.3.cloned.1.call-start = ((), (), s32[]{:S(2)}) async-start(), calls=%async_computation.2 | async-start | bytes 4718592 | tf_op jit(solution)/shard_map/reduce_scatter | solution.py:227
  8.5 1.2 copy-start.2
  9.7 1.0 copy-start.4
  10.7 97.1 %copy-start.5 = (f32[1,1,4,256,256]{4,3,2,1,0:T(8,128)S(1)}, f32[1,1,4,256,256]{4,3,2,1,0:T(8,128)}, u32[]{:S(2)}) copy-start(f32[1,1,4,256,256]{4,3,2,1,0:T(8,128)} %param.9) | copy-start | bytes 3145732
  14.5 2.0 copy-start
  16.5 171.6 %copy-start.3 = (bf16[256,2048]{1,0:T(8,128)(2,1)S(1)}, bf16[256,2048]{1,0:T(8,128)(2,1)}, u32[]{:S(2)}) copy-start(bf16[256,2048]{1,0:T(8,128)(2,1)} %acts_ref.1) | copy-start | bytes 3145732
  16.5 171.5 %all-gather.2.cloned.1.call-start = ((), (), s32[]{:S(2)}) async-start(), calls=%async_computation.3 | async-start | bytes 4718592 | tf_op jit(solution)/shard_map/all_gather | solution.py:233
  107.8 1.0 copy-start.6
  115.5 105.9 %reduce-scatter.5.cloned.1.call-start = ((), (), s32[]{:S(2)}) async-start(), calls=%async_computation.4 | async-start | bytes 655360 | tf_op jit(solution)/shard_map/reduce_scatter | solution.py:236
  188.1 2.2 copy-start.1
Sparse Core Ops, SparseCore 0:
  16.7 91.1 reduce-scatter.2
  115.6 72.4 all-gather.1
  201.1 20.1 reduce-scatter.4

commit v2 on v1

v2 whole, which is shorter than its diff:
```python
import functools

import jax
import jax.numpy as jnp
from jax import lax
from jax.experimental import pallas as pl
from jax.experimental.pallas import tpu as pltpu
from jax.sharding import PartitionSpec as P

ITERS = 6

decay_rate = 0.9
step_rate = 0.01
VMEM_BYTES = 48 * 1024 * 1024


def spot(index, count):
    if count % 2:
        return index
    odd = lax.rem(index, 2)
    half = index // 2
    return (1 - odd) * half + odd * (count - 1 - half)


def at_spot(place, count):
    place = lax.rem(place + 2 * count, count)
    if count % 2:
        return place
    far = (2 * place) // count
    return (1 - far) * (2 * place) + far * (2 * (count - place) - 1)


def refresh_kernel(
    n, slots, width, row_ref, col_ref, act_ref, cot_ref, old_ref, stats_ref, out_ref,
    act_cut, cot_cut, first_ref, acc_ref, grad_ref, mat_ref, iter_ref, gath_ref,
    rs_send, rs_recv, ag_send, ag_recv, out_sem,
):
    me = lax.axis_index("dp")
    here = spot(me, n)
    after, before = at_spot(here + 1, n), at_spot(here - 1, n)
    forward = (slots + 1) // 2
    sign = [1 if k < forward else -1 for k in range(slots)]
    turns = sorted(range(slots), key=lambda k: (k % forward, k))
    target = {1: after, -1: before}

    barrier = pltpu.get_barrier_semaphore()
    for peer in (before, after):
        pl.semaphore_signal(
            barrier, inc=1, device_id={"dp": peer}, device_id_type=pl.DeviceIdType.MESH
        )

    for r in range(act_cut.shape[0]):
        act_cut[r] = act_ref[:, r * width : (r + 1) * width]
    for c in range(cot_cut.shape[0]):
        cot_cut[c] = cot_ref[:, c * width : (c + 1) * width]

    def term(place, k):
        index = at_spot(place, n) * slots + k
        return lax.dot_general(
            act_cut[row_ref[index]],
            cot_cut[col_ref[index]],
            (((0,), (0,)), ((), ())),
            preferred_element_type=jnp.float32,
        )

    def sum_copy(k, step, first=False):
        return pltpu.make_async_remote_copy(
            src_ref=first_ref.at[k] if first else acc_ref.at[k, step - 1],
            dst_ref=acc_ref.at[k, step],
            send_sem=rs_send.at[k, step],
            recv_sem=rs_recv.at[k, step],
            device_id={"dp": target[sign[k]]},
            device_id_type=pl.DeviceIdType.MESH,
        )

    def gather_copy(k, step, owner):
        return pltpu.make_async_remote_copy(
            src_ref=gath_ref.at[owner, k],
            dst_ref=gath_ref.at[owner, k],
            send_sem=ag_send.at[k, step],
            recv_sem=ag_recv.at[k, step],
            device_id={"dp": target[sign[k]]},
            device_id_type=pl.DeviceIdType.MESH,
        )

    def out_copy(k, step, owner):
        return pltpu.make_async_copy(
            gath_ref.at[owner, k], out_ref.at[owner, k], out_sem.at[k, step]
        )

    for k in turns:
        first_ref[k] = term(here - sign[k], k).astype(jnp.bfloat16)
    pl.semaphore_wait(barrier, 2)
    for k in turns:
        sum_copy(k, 0, True).start()

    def pass_on(step, _):
        for k in turns:
            own = term(here - sign[k] * (2 + step), k)
            sum_copy(k, step, True).wait_recv()
            acc_ref[k, step] = (acc_ref[k, step].astype(jnp.float32) + own).astype(jnp.bfloat16)
            sum_copy(k, step + 1).start()
        return 0

    lax.fori_loop(0, n - 2, pass_on, 0)
    for k in turns:
        own = term(here, k)
        sum_copy(k, n - 2, True).wait_recv()
        grad_ref[k] = (acc_ref[k, n - 2].astype(jnp.float32) + own).astype(jnp.bfloat16)

    row = lax.broadcasted_iota(jnp.int32, (width, width), 0)
    col = lax.broadcasted_iota(jnp.int32, (width, width), 1)
    identity = jnp.where(row == col, 1.0, 0.0).astype(jnp.float32)
    dot = functools.partial(jnp.dot, preferred_element_type=jnp.float32)
    norms = []
    for k in range(slots):
        g = grad_ref[k]
        gram = (
            lax.dot_general(g, g, (((1,), (1,)), ((), ())), preferred_element_type=jnp.float32)
            / width
        )
        renewed = decay_rate * old_ref[k] + (1.0 - decay_rate) * gram
        stats_ref[k] = renewed
        norm = jnp.sqrt(jnp.sum(renewed * renewed, keepdims=True) + 1e-06)
        norms.append(norm)
        mat_ref[k] = renewed / norm

    def factors():
        return [((5.0 * identity - mat_ref[k]) / 4.0).astype(jnp.bfloat16) for k in range(slots)]

    def advance(low):
        square = [dot(low[k], low[k]).astype(jnp.bfloat16) for k in range(slots)]
        fourth = [dot(square[k], square[k]).astype(jnp.bfloat16) for k in range(slots)]
        for k in range(slots):
            mat_ref[k] = dot(fourth[k], mat_ref[k].astype(jnp.bfloat16))

    low = factors()
    for k in range(slots):
        iter_ref[k] = low[k]
    advance(low)

    def newton_step(step, _):
        low = factors()
        for k in range(slots):
            iter_ref[k] = dot(iter_ref[k], low[k]).astype(jnp.bfloat16)
        advance(low)
        return 0

    lax.fori_loop(1, ITERS - 1, newton_step, 0)
    low = factors()
    for k in turns:
        root = dot(iter_ref[k], low[k]) * norms[k] ** (-0.25)
        gath_ref[me, k] = dot(root.astype(jnp.bfloat16), grad_ref[k]).astype(jnp.bfloat16)
        gather_copy(k, 0, me).start()
        out_copy(k, n - 1, me).start()

    def relay(step, _):
        for k in turns:
            owner = at_spot(here - sign[k] * (1 + step), n)
            gather_copy(k, step, owner).wait_recv()
            gather_copy(k, step + 1, owner).start()
            out_copy(k, step, owner).start()
        return 0

    lax.fori_loop(0, n - 2, relay, 0)
    for k in turns:
        owner = at_spot(here - sign[k] * (n - 1), n)
        gather_copy(k, n - 2, owner).wait_recv()
        out_copy(k, n - 2, owner).start()

    def finish(step, _):
        for k in turns:
            sum_copy(k, step, True).wait_send()
            gather_copy(k, step, me).wait_send()
            out_copy(k, step, me).wait()
        return 0

    lax.fori_loop(0, n - 1, finish, 0)
    for k in turns:
        out_copy(k, n - 1, me).wait()


def refresh(n, row_of, col_of, activations, cotangent, old):
    slots, width, _ = old.shape
    tokens = activations.shape[0]
    vmem = pl.BlockSpec(memory_space=pltpu.VMEM)
    smem = pl.BlockSpec(memory_space=pltpu.SMEM)
    dma = pltpu.SemaphoreType.DMA
    low = jnp.bfloat16
    return pl.pallas_call(
        functools.partial(refresh_kernel, n, slots, width),
        out_shape=(
            jax.ShapeDtypeStruct((slots, width, width), jnp.float32),
            jax.ShapeDtypeStruct((n, slots, width, width), low),
        ),
        in_specs=[smem, smem, vmem, vmem, vmem],
        out_specs=(vmem, pl.BlockSpec(memory_space=pl.ANY)),
        scratch_shapes=[
            pltpu.VMEM((activations.shape[1] // width, tokens, width), low),
            pltpu.VMEM((cotangent.shape[1] // width, tokens, width), low),
            pltpu.VMEM((slots, width, width), low),
            pltpu.VMEM((slots, n - 1, width, width), low),
            pltpu.VMEM((slots, width, width), low),
            pltpu.VMEM((slots, width, width), jnp.float32),
            pltpu.VMEM((slots, width, width), low),
            pltpu.VMEM((n, slots, width, width), low),
            dma((slots, n - 1)),
            dma((slots, n - 1)),
            dma((slots, n - 1)),
            dma((slots, n - 1)),
            dma((slots, n)),
        ],
        compiler_params=pltpu.CompilerParams(
            vmem_limit_bytes=VMEM_BYTES, collective_id=0, has_side_effects=True
        ),
        cost_estimate=pl.CostEstimate(
            flops=2 * slots * 31 * width**3, bytes_accessed=100_000_000, transcendentals=0
        ),
        name="refresh",
    )(row_of, col_of, activations, cotangent, old)


def total_kernel(n, part_ref, out_ref, held_ref, send_sem, recv_sem):
    me = lax.axis_index("feat")
    barrier = pltpu.get_barrier_semaphore()
    for d in range(1, n):
        pl.semaphore_signal(
            barrier,
            inc=1,
            device_id={"feat": lax.rem(me + d, n)},
            device_id_type=pl.DeviceIdType.MESH,
        )
    pl.semaphore_wait(barrier, n - 1)
    copies = []
    for d in range(1, n):
        peer = lax.rem(me + d, n)
        copy = pltpu.make_async_remote_copy(
            src_ref=part_ref.at[peer],
            dst_ref=held_ref.at[d - 1],
            send_sem=send_sem.at[d - 1],
            recv_sem=recv_sem.at[d - 1],
            device_id={"feat": peer},
            device_id_type=pl.DeviceIdType.MESH,
        )
        copy.start()
        copies.append(copy)
    total = part_ref[me].astype(jnp.float32)
    for d in range(1, n):
        copies[d - 1].wait_recv()
        total = total + held_ref[d - 1].astype(jnp.float32)
    out_ref[...] = total.astype(out_ref.dtype)
    for copy in copies:
        copy.wait_send()


def total_over_feat(n, parts):
    _, tokens, cols = parts.shape
    vmem = pl.BlockSpec(memory_space=pltpu.VMEM)
    return pl.pallas_call(
        functools.partial(total_kernel, n),
        out_shape=jax.ShapeDtypeStruct((tokens, cols), parts.dtype),
        in_specs=[vmem],
        out_specs=vmem,
        scratch_shapes=[
            pltpu.VMEM((n - 1, tokens, cols), parts.dtype),
            pltpu.SemaphoreType.DMA((n - 1,)),
            pltpu.SemaphoreType.DMA((n - 1,)),
        ],
        compiler_params=pltpu.CompilerParams(collective_id=1, has_side_effects=True),
        name="total_over_feat",
    )(parts)


def apply_kernel(width, col_blocks, splits, place_ref, weight_ref, acts_ref, gath_ref, new_ref, part_ref, acc_ref):
    r = pl.program_id(0)

    @pl.when(r == 0)
    def _():
        acc_ref[...] = jnp.zeros_like(acc_ref)

    for c in range(col_blocks):
        cols = slice(c * width, (c + 1) * width)
        update = gath_ref[place_ref[r * col_blocks + c]]
        fresh = weight_ref[:, cols] - step_rate * update.astype(jnp.float32)
        new_ref[:, cols] = fresh
        acc_ref[:, cols] += jnp.dot(
            acts_ref[...], fresh.astype(jnp.bfloat16), preferred_element_type=jnp.float32
        )

    @pl.when(r == pl.num_programs(0) - 1)
    def _():
        share = acc_ref.shape[1] // splits
        for f in range(splits):
            part_ref[f] = acc_ref[:, f * share : (f + 1) * share].astype(part_ref.dtype)


def apply_update(place, weight, acts, gathered, splits):
    width = gathered.shape[-1]
    rows, cols = weight.shape
    tokens = acts.shape[0]
    share = cols // splits
    return pl.pallas_call(
        functools.partial(apply_kernel, width, cols // width, splits),
        out_shape=(
            jax.ShapeDtypeStruct((rows, cols), jnp.float32),
            jax.ShapeDtypeStruct((splits, tokens, share), jnp.bfloat16),
        ),
        grid_spec=pltpu.PrefetchScalarGridSpec(
            num_scalar_prefetch=1,
            grid=(rows // width,),
            in_specs=[
                pl.BlockSpec((width, cols), lambda i, p: (i, 0)),
                pl.BlockSpec((tokens, width), lambda i, p: (0, i)),
                pl.BlockSpec(
                    gathered.shape, lambda i, p: (0, 0, 0), pipeline_mode=pl.Buffered(1)
                ),
            ],
            out_specs=(
                pl.BlockSpec((width, cols), lambda i, p: (i, 0)),
                pl.BlockSpec((splits, tokens, share), lambda i, p: (0, 0, 0)),
            ),
            scratch_shapes=[pltpu.VMEM((tokens, cols), jnp.float32)],
        ),
        compiler_params=pltpu.CompilerParams(vmem_limit_bytes=VMEM_BYTES),
        cost_estimate=pl.CostEstimate(
            flops=2 * rows * cols * tokens,
            bytes_accessed=8 * rows * cols + 2 * gathered.size,
            transcendentals=0,
        ),
        name="apply_update",
    )(place, weight, acts, gathered)


def body(n_dp, n_feat, activations, cotangent, weight, stats_old, owners, next_acts):
    width = stats_old.shape[-1]
    slots = stats_old.shape[2]
    rows_dev, columns = weight.shape
    row_blocks = rows_dev // width
    col_blocks = columns // width
    block_count = row_blocks * col_blocks
    feat_index = lax.axis_index("feat")
    data_index = lax.axis_index("dp")
    own_list = lax.dynamic_slice_in_dim(owners, feat_index * row_blocks, row_blocks, 0).reshape(
        block_count
    )
    ids = jnp.arange(block_count, dtype=jnp.int32)
    slot_of = jnp.sum(
        ((own_list[:, None] == own_list[None, :]) & (ids[None, :] < ids[:, None])).astype(jnp.int32),
        axis=1,
    )
    place = own_list * slots + slot_of
    held = place[None, :] == jnp.arange(n_dp * slots, dtype=jnp.int32)[:, None]
    order = jnp.sum(jnp.where(held, ids[None, :], 0), axis=1)
    stats, gathered = refresh(
        n_dp, order // col_blocks, order % col_blocks, activations, cotangent, stats_old[0, 0]
    )
    if n_dp * slots != block_count:
        mine = (own_list == data_index)[None, :] & (slot_of[None, :] == jnp.arange(slots)[:, None])
        stats = jnp.where(jnp.any(mine, axis=1)[:, None, None], stats, 0.0)
    gathered = gathered.reshape(n_dp * slots, width, width)
    direct = columns % (128 * n_feat) == 0
    weight_new, parts = apply_update(
        place, weight, next_acts, gathered, n_feat if direct else 1
    )
    if direct:
        next_out = total_over_feat(n_feat, parts)
    else:
        next_out = lax.psum_scatter(parts[0], "feat", scatter_dimension=1, tiled=True)
    return (weight_new, stats[None, None], next_out)


def solution(mesh):
    placed = (
        P("dp", "feat"),
        P("dp", None),
        P("feat", None),
        P("feat", "dp", None, None, None),
        P(),
        P("dp", "feat"),
    )
    return jax.shard_map(
        functools.partial(body, mesh.shape["dp"], mesh.shape["feat"]),
        mesh=mesh,
        in_specs=placed,
        out_specs=(P("feat", None), P("feat", "dp", None, None, None), P("dp", "feat")),
        check_vma=False,
    )
```

time: 228 us -> 125 us (0.55)
  waiting for transfers between devices: 184 us -> 0 us
  Pallas kernels: 21.1 us -> 113 us
  between operations: 13.8 us -> 0.71 us
    reduce_scatter x2 -> x0, waiting for transfers between devices: 111 us -> none  [the longest x1 91.1 us: body(): sums.append(lax.psum_scatter(part, 'dp', scatter_dimension=0, tiled=True))]
    pallas_call x3, Pallas kernels: 21.1 us -> 113 us  [the longest x1 93.3 us: refresh(): pl.pallas_call(functools.partial(refresh_kernel, n, slots, width), out_sh...]
    all_gather x1 -> x0, waiting for transfers between devices: 72.3 us -> none  [body(): gathered.append(lax.all_gather(update, 'dp', axis=0, tiled=True))]
    unnamed x14 -> x16, local copies, waits for them, and re-layouts: 7.51 us -> 9.67 us
  transfers between devices with their start and end apart: 3 -> 0, of which waited for: 3 -> 0; matrix products, arithmetic and copies ran while one was open for 0% -> 0% of each run, Pallas kernels for 0% -> 0%
where the time goes in v2:
time: 125 us; the launch traced here: 124 us
  Pallas kernels  113 us (90%)
  local copies, waits for them, and re-layouts  9.91 us (8%)
    pallas_call x1, Pallas kernels, refresh(): pl.pallas_call(functools.partial(refresh_kernel, n, slots, width), out_sh...  93.3 us
    pallas_call x1, Pallas kernels, apply_update(): pl.pallas_call(functools.partial(apply_kernel, width, cols // width, spli...  10.6 us
    unnamed x16, local copies, waits for them, and re-layouts  9.67 us
    pallas_call x1, Pallas kernels, total_over_feat(): pl.pallas_call(functools.partial(total_kernel, n), out_shape=jax.ShapeDty...  9.4 us

profile of v2, /device:TPU:0, one launch (start us, length us, event | category | flops | bytes accessed | tf_op | source)
XLA Modules:
  0.0 124.2 jit_solution(10693318358560159388)
XLA Ops:
  0.6 0.0 copy-start
  0.6 0.0 copy-start.2
  0.7 0.7 copy-done
  1.3 0.1 constant_dynamic-slice_fusion
  1.4 0.1 copy.11
  1.5 0.1 reshape.22
  1.6 0.2 convert_reduce_fusion
  1.7 0.1 select_reduce_fusion
  1.9 0.0 copy-start.4
  1.9 1.2 copy-done.4
  3.1 0.0 copy-start.5
  3.1 1.2 copy-done.5
  4.3 0.0 copy-start.6
  4.3 1.0 copy-done.6
  5.4 93.3 %refresh.1 = (f32[4,256,256]{2,1,0:T(8,128)S(1)}, bf16[8,4,256,256]{3,2,1,0:T(8,128)(2,1)}) custom-call(s32[32]{0:T(128)S(1)} %get-tuple-element.12.row_ref, s32[32]{0:T(128)S(1)} %get-tuple-element.11.col_ref, bf16[256,2048]{1,0:T(8,128)(2,1)S(1)} %copy-done.4, bf16[256,1024]{1,0:T(8,128)(2,1)S(1)} %copy-done.6, f32[4,256,256]{2,1,0:T(8,128)S(1)} %bitcast.5), custom_call_target="tpu_custom_call" | custom-call | flops 4160749568 | bytes 100000000 | tf_op jit(solution)/shard_map/refresh/pallas_call | solution.py:190
  98.7 0.0 copy-done.2
  98.7 0.0 copy-start.1
  98.7 2.2 %copy-done.1 = bf16[8,4,256,256]{3,2,1,0:T(8,128)(2,1)S(1)} copy-done((bf16[8,4,256,256]{3,2,1,0:T(8,128)(2,1)S(1)}, bf16[8,4,256,256]{3,2,1,0:T(8,128)(2,1)}, u32[]{:S(2)}) %copy-start.1) | copy-done | bytes 4194328
  100.9 10.6 %apply_update.1 = (f32[2048,1024]{1,0:T(8,128)}, bf16[4,256,256]{2,1,0:T(8,128)(2,1)S(1)}) custom-call(s32[32]{0:T(128)S(1)} %multiply_add_fusion.place_ref, f32[2048,1024]{1,0:T(8,128)} %weight_ref.1, bf16[256,2048]{1,0:T(8,128)(2,1)S(1)} %copy-done.2, bf16[32,256,256]{2,1,0:T(8,128)(2,1)S(1)} %bitcast.3), custom_call_target="tpu_custom_call" | custom-call | flops 1073741824 | bytes 20971520 | tf_op jit(solution)/shard_map/apply_update/pallas_call | solution.py:302
  111.5 0.0 copy-start.3
  111.5 0.8 copy-done.3
  112.3 9.4 %total_over_feat.1 = bf16[256,256]{1,0:T(8,128)(2,1)} custom-call(bf16[4,256,256]{2,1,0:T(8,128)(2,1)} %copy-done.3), custom_call_target="tpu_custom_call" | custom-call | tf_op jit(solution)/shard_map/total_over_feat/pallas_call | solution.py:259
  121.7 1.0 copy.14
  122.7 1.6 %copy.15 = bf16[256,256]{1,0:T(8,128)(2,1)} copy(bf16[256,256]{1,0:T(8,128)(2,1)} %total_over_feat.1) | data formatting | bytes 262144
  (2 shorter events, 0.0 us)
Async XLA Ops:
  0.6 0.7 copy-start
  0.6 98.1 %copy-start.2 = (bf16[256,2048]{1,0:T(8,128)(2,1)S(1)}, bf16[256,2048]{1,0:T(8,128)(2,1)}, u32[]{:S(2)}) copy-start(bf16[256,2048]{1,0:T(8,128)(2,1)} %acts_ref.1) | copy-start | bytes 3145732
  1.9 1.2 copy-start.4
  3.1 1.2 copy-start.5
  4.3 1.0 copy-start.6
  98.7 2.2 %copy-start.1 = (bf16[8,4,256,256]{3,2,1,0:T(8,128)(2,1)S(1)}, bf16[8,4,256,256]{3,2,1,0:T(8,128)(2,1)}, u32[]{:S(2)}) copy-start(bf16[8,4,256,256]{3,2,1,0:T(8,128)(2,1)} %get-tuple-element.7) | copy-start | bytes 12582916
  111.5 0.8 copy-start.3

commit v3 on v2

--- a/solution.py
+++ b/solution.py
@@ -12,6 +12,9 @@
 decay_rate = 0.9
 step_rate = 0.01
 VMEM_BYTES = 48 * 1024 * 1024
+REFRESH_BYTES = 20 * 1024 * 1024
+APPLY_BYTES = 16 * 1024 * 1024
+TOTAL_BYTES = 4 * 1024 * 1024
 
 
 def spot(index, count):
@@ -31,9 +34,9 @@
 
 
 def refresh_kernel(
-    n, slots, width, row_ref, col_ref, act_ref, cot_ref, old_ref, stats_ref, out_ref,
-    act_cut, cot_cut, first_ref, acc_ref, grad_ref, mat_ref, iter_ref, gath_ref,
-    rs_send, rs_recv, ag_send, ag_recv, out_sem,
+    n, slots, width, row_ref, col_ref, act_ref, cot_ref, old_hbm, stats_ref, gath_ref,
+    act_cut, cot_cut, old_ref, first_ref, acc_ref, grad_ref, mat_ref, iter_ref,
+    rs_send, rs_recv, ag_send, ag_recv, act_sem, cot_sem, old_sem,
 ):
     me = lax.axis_index("dp")
     here = spot(me, n)
@@ -49,10 +52,21 @@
             barrier, inc=1, device_id={"dp": peer}, device_id_type=pl.DeviceIdType.MESH
         )
 
-    for r in range(act_cut.shape[0]):
-        act_cut[r] = act_ref[:, r * width : (r + 1) * width]
-    for c in range(cot_cut.shape[0]):
-        cot_cut[c] = cot_ref[:, c * width : (c + 1) * width]
+    cuts = [
+        pltpu.make_async_copy(
+            cot_ref.at[:, c * width : (c + 1) * width], cot_cut.at[c], cot_sem.at[c]
+        )
+        for c in range(cot_cut.shape[0])
+    ] + [
+        pltpu.make_async_copy(
+            act_ref.at[:, r * width : (r + 1) * width], act_cut.at[r], act_sem.at[r]
+        )
+        for r in range(act_cut.shape[0])
+    ]
+    load_old = pltpu.make_async_copy(old_hbm, old_ref, old_sem)
+    for cut in cuts:
+        cut.start()
+    load_old.start()
 
     def term(place, k):
         index = at_spot(place, n) * slots + k
@@ -83,11 +97,8 @@
             device_id_type=pl.DeviceIdType.MESH,
         )
 
-    def out_copy(k, step, owner):
-        return pltpu.make_async_copy(
-            gath_ref.at[owner, k], out_ref.at[owner, k], out_sem.at[k, step]
-        )
-
+    for cut in cuts:
+        cut.wait()
     for k in turns:
         first_ref[k] = term(here - sign[k], k).astype(jnp.bfloat16)
     pl.semaphore_wait(barrier, 2)
@@ -108,6 +119,7 @@
         sum_copy(k, n - 2, True).wait_recv()
         grad_ref[k] = (acc_ref[k, n - 2].astype(jnp.float32) + own).astype(jnp.bfloat16)
 
+    load_old.wait()
     row = lax.broadcasted_iota(jnp.int32, (width, width), 0)
     col = lax.broadcasted_iota(jnp.int32, (width, width), 1)
     identity = jnp.where(row == col, 1.0, 0.0).astype(jnp.float32)
@@ -152,32 +164,26 @@
         root = dot(iter_ref[k], low[k]) * norms[k] ** (-0.25)
         gath_ref[me, k] = dot(root.astype(jnp.bfloat16), grad_ref[k]).astype(jnp.bfloat16)
         gather_copy(k, 0, me).start()
-        out_copy(k, n - 1, me).start()
 
     def relay(step, _):
         for k in turns:
             owner = at_spot(here - sign[k] * (1 + step), n)
             gather_copy(k, step, owner).wait_recv()
             gather_copy(k, step + 1, owner).start()
-            out_copy(k, step, owner).start()
         return 0
 
     lax.fori_loop(0, n - 2, relay, 0)
     for k in turns:
         owner = at_spot(here - sign[k] * (n - 1), n)
         gather_copy(k, n - 2, owner).wait_recv()
-        out_copy(k, n - 2, owner).start()
 
     def finish(step, _):
         for k in turns:
             sum_copy(k, step, True).wait_send()
             gather_copy(k, step, me).wait_send()
-            out_copy(k, step, me).wait()
         return 0
 
     lax.fori_loop(0, n - 1, finish, 0)
-    for k in turns:
-        out_copy(k, n - 1, me).wait()
 
 
 def refresh(n, row_of, col_of, activations, cotangent, old):
@@ -185,6 +191,7 @@
     tokens = activations.shape[0]
     vmem = pl.BlockSpec(memory_space=pltpu.VMEM)
     smem = pl.BlockSpec(memory_space=pltpu.SMEM)
+    hbm = pl.BlockSpec(memory_space=pltpu.HBM)
     dma = pltpu.SemaphoreType.DMA
     low = jnp.bfloat16
     return pl.pallas_call(
@@ -193,25 +200,29 @@
             jax.ShapeDtypeStruct((slots, width, width), jnp.float32),
             jax.ShapeDtypeStruct((n, slots, width, width), low),
         ),
-        in_specs=[smem, smem, vmem, vmem, vmem],
-        out_specs=(vmem, pl.BlockSpec(memory_space=pl.ANY)),
+        in_specs=[smem, smem, hbm, hbm, hbm],
+        out_specs=(vmem, vmem),
         scratch_shapes=[
             pltpu.VMEM((activations.shape[1] // width, tokens, width), low),
             pltpu.VMEM((cotangent.shape[1] // width, tokens, width), low),
+            pltpu.VMEM((slots, width, width), jnp.float32),
             pltpu.VMEM((slots, width, width), low),
             pltpu.VMEM((slots, n - 1, width, width), low),
             pltpu.VMEM((slots, width, width), low),
             pltpu.VMEM((slots, width, width), jnp.float32),
             pltpu.VMEM((slots, width, width), low),
-            pltpu.VMEM((n, slots, width, width), low),
             dma((slots, n - 1)),
             dma((slots, n - 1)),
             dma((slots, n - 1)),
             dma((slots, n - 1)),
-            dma((slots, n)),
+            dma((activations.shape[1] // width,)),
+            dma((cotangent.shape[1] // width,)),
+            dma,
         ],
         compiler_params=pltpu.CompilerParams(
-            vmem_limit_bytes=VMEM_BYTES, collective_id=0, has_side_effects=True
+            vmem_limit_bytes=REFRESH_BYTES if n * slots <= 32 else VMEM_BYTES,
+            collective_id=0,
+            has_side_effects=True,
         ),
         cost_estimate=pl.CostEstimate(
             flops=2 * slots * 31 * width**3, bytes_accessed=100_000_000, transcendentals=0
@@ -266,7 +277,9 @@
             pltpu.SemaphoreType.DMA((n - 1,)),
             pltpu.SemaphoreType.DMA((n - 1,)),
         ],
-        compiler_params=pltpu.CompilerParams(collective_id=1, has_side_effects=True),
+        compiler_params=pltpu.CompilerParams(
+            vmem_limit_bytes=TOTAL_BYTES, collective_id=1, has_side_effects=True
+        ),
         name="total_over_feat",
     )(parts)
 
@@ -321,7 +334,7 @@
             ),
             scratch_shapes=[pltpu.VMEM((tokens, cols), jnp.float32)],
         ),
-        compiler_params=pltpu.CompilerParams(vmem_limit_bytes=VMEM_BYTES),
+        compiler_params=pltpu.CompilerParams(vmem_limit_bytes=APPLY_BYTES if gathered.size <= 1 << 21 else VMEM_BYTES),
         cost_estimate=pl.CostEstimate(
             flops=2 * rows * cols * tokens,
             bytes_accessed=8 * rows * cols + 2 * gathered.size,

time: 125 us -> 115 us (0.920)
  Pallas kernels: 113 us -> 107 us
  local copies, waits for them, and re-layouts: 9.91 us -> 6.18 us
    pallas_call x1, Pallas kernels: 10.6 us -> 6.48 us  [apply_update(): pl.pallas_call(functools.partial(apply_kernel, width, cols // width, spli...]
    unnamed x16, local copies, waits for them, and re-layouts: 9.67 us -> 5.94 us
    pallas_call x1, Pallas kernels: 9.4 us -> 7.69 us  [total_over_feat(): pl.pallas_call(functools.partial(total_kernel, n), out_shape=jax.ShapeDty...]
where the time goes in v3:
time: 115 us; the launch traced here: 114 us
  Pallas kernels  107 us (93%)
  local copies, waits for them, and re-layouts  6.18 us (5%)
    pallas_call x1, Pallas kernels, refresh(): pl.pallas_call(functools.partial(refresh_kernel, n, slots, width), out_sh...  92.6 us
    pallas_call x1, Pallas kernels, total_over_feat(): pl.pallas_call(functools.partial(total_kernel, n), out_shape=jax.ShapeDty...  7.69 us
    pallas_call x1, Pallas kernels, apply_update(): pl.pallas_call(functools.partial(apply_kernel, width, cols // width, spli...  6.48 us
    unnamed x16, local copies, waits for them, and re-layouts  5.94 us

profile of v3, /device:TPU:0, one launch (start us, length us, event | category | flops | bytes accessed | tf_op | source)
XLA Modules:
  0.0 114.0 jit_solution(4309737403246512769)
XLA Ops:
  0.6 0.0 copy-start
  0.6 0.0 copy-start.1
  0.7 0.7 copy-done
  1.3 0.1 constant_dynamic-slice_fusion
  1.4 0.1 copy.11
  1.5 0.1 reshape.22
  1.6 0.0 slice-start
  1.6 0.2 convert_reduce_fusion
  1.7 0.1 select_reduce_fusion
  1.9 0.0 copy-start.2
  1.9 1.4 %copy-done.2 = bf16[256,2048]{1,0:T(8,128)(2,1)S(1)} copy-done((bf16[256,2048]{1,0:T(8,128)(2,1)S(1)}, bf16[256,2048]{1,0:T(8,128)(2,1)}, u32[]{:S(2)}) %copy-start.2) | copy-done | bytes 1048600
  3.3 0.0 copy-start.3
  3.3 1.2 %copy-done.3 = f32[1,1,4,256,256]{4,3,2,1,0:T(8,128)S(1)} copy-done((f32[1,1,4,256,256]{4,3,2,1,0:T(8,128)S(1)}, f32[1,1,4,256,256]{4,3,2,1,0:T(8,128)}, u32[]{:S(2)}) %copy-start.3) | copy-done | bytes 1048600
  4.5 0.0 copy-start.4
  4.5 1.0 copy-done.4
  5.5 0.0 slice-start.1
  5.5 92.6 %refresh.1 = (f32[4,256,256]{2,1,0:T(8,128)S(1)}, bf16[8,4,256,256]{3,2,1,0:T(8,128)(2,1)S(1)}) custom-call(s32[32]{0:T(128)S(1)} %get-tuple-element.12.row_ref, s32[32]{0:T(128)S(1)} %get-tuple-element.11.col_ref, bf16[256,2048]{1,0:T(8,128)(2,1)S(1)} %copy-done.2, bf16[256,1024]{1,0:T(8,128)(2,1)S(1)} %copy-done.4, f32[4,256,256]{2,1,0:T(8,128)S(1)} %bitcast.7), custom_call_target="tpu_custom_call" | custom-call | flops 4160749568 | bytes 100000000 | tf_op jit(solution)/shard_map/refresh/pallas_call | solution.py:197
  98.2 0.0 copy-done.1
  98.2 0.0 slice-done
  98.2 0.0 slice-done.1
  98.2 6.5 %apply_update.1 = (f32[2048,1024]{1,0:T(8,128)}, bf16[4,256,256]{2,1,0:T(8,128)(2,1)S(1)}) custom-call(s32[32]{0:T(128)S(1)} %multiply_add_fusion.place_ref, f32[2048,1024]{1,0:T(8,128)S(1)} %bitcast.4, bf16[256,2048]{1,0:T(8,128)(2,1)S(1)} %copy-done.1, bf16[32,256,256]{2,1,0:T(8,128)(2,1)S(1)} %bitcast.5), custom_call_target="tpu_custom_call" | custom-call | flops 1073741824 | bytes 20971520 | tf_op jit(solution)/shard_map/apply_update/pallas_call | solution.py:315
  104.7 7.7 %total_over_feat.1 = bf16[256,256]{1,0:T(8,128)(2,1)S(1)} custom-call(bf16[4,256,256]{2,1,0:T(8,128)(2,1)S(1)} %get-tuple-element.10.part_ref), custom_call_target="tpu_custom_call" | custom-call | tf_op jit(solution)/shard_map/total_over_feat/pallas_call | solution.py:270
  112.4 1.0 copy.14
  113.3 0.7 copy.15
  (3 shorter events, 0.0 us)
Async XLA Ops:
  0.6 0.7 copy-start
  0.6 97.5 %copy-start.1 = (bf16[256,2048]{1,0:T(8,128)(2,1)S(1)}, bf16[256,2048]{1,0:T(8,128)(2,1)}, u32[]{:S(2)}) copy-start(bf16[256,2048]{1,0:T(8,128)(2,1)} %acts_ref.1) | copy-start | bytes 3145732
  1.6 96.6 %slice-start = ((s8[8388608]{0:T(1024)(128)(4,1)}), s8[4194304]{0:T(1024)(128)(4,1)S(1)}, s32[]{:S(2)}) async-start(s8[8388608]{0:T(1024)(128)(4,1)} %bitcast.3), calls=%async_computation | async-start | bytes 8388608
  1.9 1.4 %copy-start.2 = (bf16[256,2048]{1,0:T(8,128)(2,1)S(1)}, bf16[256,2048]{1,0:T(8,128)(2,1)}, u32[]{:S(2)}) copy-start(bf16[256,2048]{1,0:T(8,128)(2,1)} %act_ref.1) | copy-start | bytes 3145732
  3.3 1.2 %copy-start.3 = (f32[1,1,4,256,256]{4,3,2,1,0:T(8,128)S(1)}, f32[1,1,4,256,256]{4,3,2,1,0:T(8,128)}, u32[]{:S(2)}) copy-start(f32[1,1,4,256,256]{4,3,2,1,0:T(8,128)} %param.9) | copy-start | bytes 3145732
  4.5 1.0 copy-start.4
  5.5 92.6 %slice-start.1 = ((s8[8388608]{0:T(1024)(128)(4,1)}), s8[4194304]{0:T(1024)(128)(4,1)S(1)}, s32[]{:S(2)}) async-start(s8[8388608]{0:T(1024)(128)(4,1)} %bitcast.3), calls=%async_computation.1 | async-start | bytes 8388608
